TPU v7x, 32 devices: a whole 2x2x4 slice. The times are simulated.
32 devices in a mesh: track: 16 (over z, y, x), cam: 2 (over core).
Axes of the slice: x: 2, y: 2, z: 4, core: 2. Of those that a mesh axis runs over, the one named last changes fastest.
Arguments:
- omega: bfloat16 [32, 9, 4096], P(None, None, ('track', 'cam')), may hold values from -6 to 6
- u_blocks: float32 [9, 9, 4096], P(None, None, ('track', 'cam')), may hold values from -5.4 to 36, as said below
- w_blocks: bfloat16 [9, 3, 16384], P(None, None, ('track', 'cam')), may hold values from -1.796875 to 1.796875
- v_inverse: float32 [3, 3, 4096], P(None, None, ('track', 'cam')), may hold values from -0.6 to 1.5, as said below
- obs_camera: int32 [16384], P(('track', 'cam')), may hold values from 0 to 4095, as said below
- obs_track: int32 [16384], P(('track', 'cam')), may hold values from 0 to 31, as said below
- obs_mask: int32 [16384], P(('track', 'cam')), may hold values from 0 to 1, as said below
Outputs:
- sketch: float32 [32, 9, 4096], P(None, None, ('track', 'cam'))
- basis: float32 [32, 9, 4096], P(None, None, ('track', 'cam'))
- factor: float32 [32, 32], replicated
Inputs may be any that keep to these rules, and one draw needn't show every extreme that they name: `obs_camera`: cameras c * 128 to (c + 1) * 128 - 1 belong to device c (track slower). Among one device's 512 observations, padding included, at most 32 name cameras of any one device, and exactly 32 name those of some device. `obs_track`: in each aligned block of 128 observations, slots 0 to 31 each hold one track of 2 to 4 consecutive observations from the block's start, in rising order; the padding after them carries slot 31. `obs_mask`: 1 on the observations of tracks, 0 on the padding at the end of each block. `u_blocks`: each block is symmetric. `v_inverse`: each block is symmetric positive definite.
All inputs are finite; a program needn't handle non-finite values.
Results may differ from a plain program's by a relative error of at most 0.00095.
Values may be sent and summed in bfloat16 or wider, within the bound.
A program may use at most 64 MiB of HBM per device.

v0:
```python
import functools

import jax
import jax.numpy as jnp
from jax import lax
from jax.experimental import pallas as pl
from jax.experimental.pallas import tpu as pltpu
from jax.sharding import PartitionSpec as P

BLK_OBS = 128
TRK_BLK = 32
LANES = 128
CHUNK = 1024

HIGH = lax.Precision.HIGHEST
MESH = pl.DeviceIdType.MESH
NT = (((1,), (1,)), ((), ()))
F32 = jnp.float32
BF16 = jnp.bfloat16


def dot(left, right, precision=None):
    return jnp.dot(left, right, precision=precision, preferred_element_type=F32)


def dot_nt(left, right, precision=None):
    return lax.dot_general(left, right, NT, precision=precision, preferred_element_type=F32)


def one_hot(condition):
    return jnp.where(condition, 1.0, 0.0).astype(BF16)


def rows_iota(shape):
    return lax.broadcasted_iota(jnp.int32, shape, 0)


def lanes_iota(shape):
    return lax.broadcasted_iota(jnp.int32, shape, 1)


def repeat(count, body):
    if count == 1:
        body(0)
    else:
        pl.loop(0, count)(body)


def kernel(
    sizes,
    omega_hbm, u_hbm, w_hbm, v_hbm, camera_hbm, track_hbm, mask_hbm,
    sketch_ref, basis_ref, factor_ref,
    send1, recv1, send2, recv2, send3, recv3, gsend, grecv,
    fields, to_track, wide, pick, own, incoming, sum_ref,
    send_sems, recv_sems,
    omega_ref, u_ref, w_ref, v_ref, camera_ref, track_ref, mask_ref, load_sems,
):
    track_count, cam_count, params, columns, rows, groups, span = sizes
    devices = track_count * cam_count
    cam_width = omega_ref.shape[1]
    obs_count = camera_ref.shape[1]
    tracks = v_ref.shape[2]
    part_rows = span * rows
    chunk = groups * part_rows
    chunks = devices // span
    me = lax.axis_index("track") * cam_count + lax.axis_index("cam")

    def peer(turn):
        other = lax.rem(me + turn + 1, devices)
        return other, (other // cam_count, lax.rem(other, cam_count))

    barrier = pltpu.get_barrier_semaphore()

    @pl.loop(0, devices - 1)
    def _(turn):
        pl.semaphore_signal(barrier, inc=1, device_id=peer(turn)[1], device_id_type=MESH)

    loads = [
        pltpu.make_async_copy(source, target, load_sems.at[index])
        for index, (source, target) in enumerate(
            [
                (camera_hbm, camera_ref),
                (track_hbm, track_ref),
                (mask_hbm, mask_ref),
                (w_hbm, w_ref),
                (omega_hbm, omega_ref),
                (u_hbm, u_ref),
                (v_hbm, v_ref),
            ]
        )
    ]
    for load in loads:
        load.start()

    def scatter(index, src, dst):
        @pl.loop(0, devices - 1)
        def _(turn):
            other, where = peer(turn)
            pltpu.make_async_remote_copy(
                src_ref=src.at[other],
                dst_ref=dst.at[me],
                send_sem=send_sems.at[index],
                recv_sem=recv_sems.at[index],
                device_id=where,
                device_id_type=MESH,
            ).start()

        pltpu.make_async_copy(src.at[me], dst.at[me], recv_sems.at[index]).start()

    def broadcast(index, src, dst):
        @pl.loop(0, devices - 1)
        def _(turn):
            pltpu.make_async_remote_copy(
                src_ref=src,
                dst_ref=dst.at[me],
                send_sem=send_sems.at[index],
                recv_sem=recv_sems.at[index],
                device_id=peer(turn)[1],
                device_id_type=MESH,
            ).start()

        pltpu.make_async_copy(src, dst.at[me], recv_sems.at[index]).start()

    def arrive(index, dst):
        pltpu.make_async_copy(dst, dst, recv_sems.at[index]).wait()

    def sent(index, dst):
        part = dst.at[pl.ds(0, devices - 1)]
        pltpu.make_async_copy(part, part, send_sems.at[index]).wait()

    eye = one_hot(rows_iota((LANES, LANES)) == lanes_iota((LANES, LANES)))

    def pack(part, values, dst):
        for index in range(values.shape[0] // columns):
            block = values[index * columns : (index + 1) * columns]
            pieces = [block[:, g * part_rows : (g + 1) * part_rows] for g in range(groups)]
            if groups * columns < LANES:
                pieces.append(jnp.zeros((LANES - groups * columns, part_rows), F32))
            turned = jnp.concatenate(pieces, axis=0).T.reshape(span, rows, LANES)
            dst[pl.ds(part * span, span), index * rows : (index + 1) * rows] = turned.astype(BF16)

    def unpack(part, src):
        blocks = []
        for index in range(src.shape[1] // rows):
            block = src[pl.ds(part * span, span), index * rows : (index + 1) * rows]
            turned = dot_nt(eye, block.reshape(part_rows, LANES))
            blocks.append(
                jnp.concatenate(
                    [turned[g * columns : (g + 1) * columns] for g in range(groups)], axis=1
                )
            )
        return jnp.concatenate(blocks, axis=0)

    for load in loads[:4]:
        load.wait()
    camera = camera_ref[...]
    owner = camera // cam_width
    local = camera - owner * cam_width
    track_id = lanes_iota((1, obs_count)) // BLK_OBS * TRK_BLK + track_ref[...]
    live = mask_ref[...].astype(F32)
    fields[...] = jnp.zeros_like(fields)
    for row in range(params):
        fields[3 * row : 3 * row + 3, :] = w_ref[row].astype(F32) * live
    high = local // 256
    fields[3 * params : 3 * params + 1, :] = high.astype(F32)
    fields[3 * params + 1 : 3 * params + 2, :] = (local - high * 256).astype(F32)
    owned = one_hot(rows_iota((devices, obs_count)) == owner)
    earlier = one_hot(rows_iota((obs_count, obs_count)) < lanes_iota((obs_count, obs_count)))
    ranks = dot(owned, earlier)
    rank = jnp.sum(ranks * owned.astype(F32), axis=0, keepdims=True).astype(jnp.int32)
    group = jnp.zeros_like(rank)
    for g in range(1, groups):
        group += jnp.where(rank >= g * rows, 1, 0)
    offset = group * part_rows + rank - group * rows
    member = one_hot(rows_iota((tracks, obs_count)) == track_id)
    table = jnp.concatenate([fields[...].astype(BF16), member], axis=0)

    def place(part):
        nearby = owner - part * span
        inside = jnp.logical_and(nearby >= 0, nearby < span)
        slot = jnp.where(inside, nearby * rows + offset, -1)
        slots = one_hot(rows_iota((chunk, obs_count)) == slot)
        placed = dot_nt(table, slots)
        pack(part, placed[:columns], send1)
        to_track[part] = placed[columns:].astype(BF16)

    repeat(chunks, place)

    pl.semaphore_wait(barrier, devices - 1)
    scatter(0, send1, recv1)

    for load in loads[4:]:
        load.wait()
    for row in range(params):
        total = jnp.zeros((columns, cam_width), F32)
        for col in range(params):
            total += u_ref[row, col : col + 1, :] * omega_ref[
                col * columns : (col + 1) * columns, :
            ].astype(F32)
        own[row * columns : (row + 1) * columns, :] = total
    incoming[...] = jnp.zeros_like(incoming)
    sum_ref[...] = jnp.zeros_like(sum_ref)

    def project(part):
        turned = unpack(part, recv1)
        wide[part] = turned
        number = turned[3 * params : 3 * params + 1] * 256.0 + turned[
            3 * params + 1 : 3 * params + 2
        ]
        chosen = one_hot(rows_iota((cam_width, chunk)) == number.astype(jnp.int32))
        pick[part] = chosen
        gathered = dot(omega_ref[...], chosen)
        pieces = []
        for comp in range(3):
            total = jnp.zeros((columns, chunk), F32)
            for row in range(params):
                at = row * 3 + comp
                total += turned[at : at + 1] * gathered[row * columns : (row + 1) * columns]
            pieces.append(total)
        pack(part, jnp.concatenate(pieces, axis=0), send2)

    arrive(0, recv1)
    repeat(chunks, project)
    scatter(1, send2, recv2)

    def collect(part):
        sum_ref[...] += dot_nt(unpack(part, recv2).astype(BF16), to_track[part])

    arrive(1, recv2)
    repeat(chunks, collect)
    pieces = []
    for row in range(3):
        total = jnp.zeros((columns, tracks), F32)
        for col in range(3):
            total += v_ref[row, col : col + 1, :] * sum_ref[col * columns : (col + 1) * columns]
        pieces.append(total)
    solved = jnp.concatenate(pieces, axis=0).astype(BF16)

    def spread(part):
        pack(part, dot(solved, to_track[part]), send3)

    repeat(chunks, spread)
    scatter(2, send3, recv3)

    def gather_back(part):
        turned = unpack(part, recv3)
        weights = wide[part]
        pieces = []
        for row in range(params):
            total = jnp.zeros((columns, chunk), F32)
            for comp in range(3):
                at = row * 3 + comp
                total += weights[at : at + 1] * turned[comp * columns : (comp + 1) * columns]
            pieces.append(total)
        contribution = jnp.concatenate(pieces, axis=0).astype(BF16)
        incoming[...] += dot_nt(contribution, pick[part])

    arrive(2, recv3)
    repeat(chunks, gather_back)

    sketch = own[...] - incoming[...]
    sketch_ref[...] = sketch
    flat = jnp.concatenate(
        [sketch[row * columns : (row + 1) * columns] for row in range(params)], axis=1
    )
    gram = dot_nt(flat, flat, HIGH)
    folds = LANES // columns
    tall = columns // folds
    gsend[...] = jnp.concatenate(
        [gram[part * tall : (part + 1) * tall] for part in range(folds)], axis=1
    )
    broadcast(3, gsend, grecv)
    arrive(3, grecv)
    packed = jnp.sum(grecv[...], axis=0)
    gram = jnp.concatenate(
        [packed[:, part * columns : (part + 1) * columns] for part in range(folds)], axis=0
    )
    work = jnp.concatenate(
        [
            gram / (params * cam_width * devices),
            jnp.where(
                rows_iota((columns, columns)) == lanes_iota((columns, columns)), 1.0, 0.0
            ),
        ],
        axis=1,
    )
    row_ids = rows_iota((columns, 1))
    for step in range(columns - 1):
        scale = work[:, step : step + 1] * (1.0 / work[step : step + 1, step : step + 1])
        work = work - jnp.where(row_ids > step, scale, 0.0) * work[step : step + 1]
    upper = work[:, :columns]
    on_diagonal = rows_iota((columns, columns)) == lanes_iota((columns, columns))
    on_upper = rows_iota((columns, columns)) <= lanes_iota((columns, columns))
    diagonal = jnp.sum(jnp.where(on_diagonal, upper, 0.0), axis=1, keepdims=True)
    root = 1.0 / jnp.sqrt(diagonal)
    factor_ref[...] = jnp.where(on_upper, upper * root, 0.0)
    inverse = work[:, columns:] * root
    basis = dot(inverse, flat, HIGH)
    for row in range(params):
        basis_ref[row * columns : (row + 1) * columns, :] = basis[
            :, row * cam_width : (row + 1) * cam_width
        ]

    sent(0, recv1)
    sent(1, recv2)
    sent(2, recv3)
    sent(3, grecv)


def on_device(omega, u_blocks, w_blocks, v_inverse, obs_camera, obs_track, obs_mask):
    track_count = lax.axis_size("track")
    cam_count = lax.axis_size("cam")
    devices = track_count * cam_count
    columns, params, cam_width = omega.shape
    obs_count = obs_camera.shape[0]
    tracks = v_inverse.shape[2]
    capacity = max(2, 2 * obs_count // devices)
    rows = -(-capacity // (LANES // columns) // 8) * 8
    groups = -(-capacity // rows)
    span = devices
    while span * rows * groups > CHUNK and span % 2 == 0:
        span //= 2
    chunk = span * rows * groups
    chunks = devices // span

    table = omega.transpose(1, 0, 2).reshape(params * columns, cam_width)
    line = (1, obs_count)
    operands = (
        table,
        u_blocks,
        w_blocks,
        v_inverse,
        obs_camera.reshape(line),
        obs_track.reshape(line),
        obs_mask.reshape(line),
    )
    sizes = (track_count, cam_count, params, columns, rows, groups, span)
    small = pltpu.VMEM((devices, rows, LANES), BF16)
    message = pltpu.VMEM((devices, 3 * rows, LANES), BF16)
    tall = columns * columns // LANES
    sketch, basis, factor = pl.pallas_call(
        functools.partial(kernel, sizes),
        out_shape=(
            pltpu.VMEM((params * columns, cam_width), F32),
            pltpu.VMEM((params * columns, cam_width), F32),
            pltpu.VMEM((columns, columns), F32),
        ),
        in_specs=[pl.BlockSpec(memory_space=pl.ANY)] * 7,
        out_specs=(pl.BlockSpec(memory_space=pltpu.VMEM),) * 3,
        scratch_shapes=[small] * 2
        + [message] * 4
        + [
            pltpu.VMEM((tall, LANES), F32),
            pltpu.VMEM((devices, tall, LANES), F32),
            pltpu.VMEM((columns, obs_count), F32),
            pltpu.VMEM((chunks, tracks, chunk), BF16),
            pltpu.VMEM((chunks, columns, chunk), F32),
            pltpu.VMEM((chunks, cam_width, chunk), BF16),
            pltpu.VMEM((params * columns, cam_width), F32),
            pltpu.VMEM((params * columns, cam_width), F32),
            pltpu.VMEM((3 * columns, tracks), F32),
            pltpu.SemaphoreType.DMA((4,)),
            pltpu.SemaphoreType.DMA((4,)),
        ]
        + [pltpu.VMEM(array.shape, array.dtype) for array in operands]
        + [pltpu.SemaphoreType.DMA((len(operands),))],
        compiler_params=pltpu.CompilerParams(collective_id=0, has_side_effects=True),
    )(*operands)

    def unfold(array):
        return array.reshape(params, columns, cam_width).transpose(1, 0, 2)

    return (unfold(sketch), unfold(basis), factor)


def solution(mesh):
    spread = P(None, None, ("track", "cam"))
    flat = P(("track", "cam"))
    return jax.shard_map(
        on_device,
        mesh=mesh,
        in_specs=(spread,) * 4 + (flat,) * 3,
        out_specs=(spread, spread, P()),
        check_vma=False,
    )
```

profile of v0, /device:TPU:0, one launch (start us, length us, event | category | flops | bytes accessed | tf_op | source)
XLA Modules:
  0.0 37.6 jit_solution(8437861023619010490)
XLA Ops:
  0.6 35.0 %shard_map.94 = (f32[288,128]{1,0:T(8,128)S(1)}, f32[288,128]{1,0:T(8,128)S(1)}, f32[32,32]{1,0:T(8,128)S(1)}) custom-call(bf16[288,128]{1,0:T(8,128)(2,1)} %bitcast.14, f32[9,9,128]{2,1,0:T(8,128)} %u_hbm.1, bf16[9,3,512]{2,1,0:T(4,128)(2,1)} %w_hbm.1, f32[3,3,128]{2,1,0:T(4,128)} %v_hbm.1, s32[1,512]{1,0:T(1,128)} %bitcast.15, s32[1,512]{1,0:T(1,128)} %bitcast.16, ...), custom_call_target="tpu_custom_call" | custom-call | tf_op jit(solution)/shard_map/pallas_call | solution.py:341
  35.6 0.7 %copy.13 = f32[32,9,128]{2,0,1:T(8,128)} copy(f32[32,9,128]{2,0,1:T(8,128)S(1)} %bitcast.13) | data formatting | bytes 294912
  36.3 0.7 %copy.14 = f32[32,9,128]{2,0,1:T(8,128)} copy(f32[32,9,128]{2,0,1:T(8,128)S(1)} %bitcast.12) | data formatting | bytes 294912
  36.9 0.6 %copy.15 = f32[32,32]{1,0:T(8,128)} copy(f32[32,32]{1,0:T(8,128)S(1)} %get-tuple-element.11) | data formatting | bytes 8192
where the time goes:
time: 37.7 us; the launch traced here: 37.6 us
  Pallas kernels  35 us (93%)
  local copies, waits for them, and re-layouts  1.93 us (5%)
  between operations  0.64 us (2%)
    pallas_call x1, Pallas kernels, on_device(): pl.pallas_call(functools.partial(kernel, sizes), out_shape=(pltpu.VMEM((p...  35 us
    unnamed x3, local copies, waits for them, and re-layouts  1.93 us

commit v1 on v0

v1 whole, which is shorter than its diff:
```python
import functools

import jax
import jax.numpy as jnp
from jax import lax
from jax.experimental import pallas as pl
from jax.experimental.pallas import tpu as pltpu
from jax.sharding import PartitionSpec as P

BLK_OBS = 128
TRK_BLK = 32
LANES = 128
STRIP = 8
CHUNK = 512

HIGH = lax.Precision.HIGHEST
MESH = pl.DeviceIdType.MESH
NT = (((1,), (1,)), ((), ()))
F32 = jnp.float32
BF16 = jnp.bfloat16

ASK, ASK_FAR, TABLE, SUM, SUM_FAR, BACK, BACK_FAR, GRAM = range(8)


def dot(left, right, precision=None):
    return jnp.dot(left, right, precision=precision, preferred_element_type=F32)


def dot_nt(left, right, precision=None):
    return lax.dot_general(left, right, NT, precision=precision, preferred_element_type=F32)


def one_hot(condition):
    return jnp.where(condition, 1.0, 0.0).astype(BF16)


def rows_iota(shape):
    return lax.broadcasted_iota(jnp.int32, shape, 0)


def lanes_iota(shape):
    return lax.broadcasted_iota(jnp.int32, shape, 1)


def repeat(count, body):
    if count == 1:
        body(0)
    else:
        pl.loop(0, count)(body)


def kernel(
    sizes,
    omega_hbm, u_hbm, w_hbm, v_hbm, camera_hbm, track_hbm, mask_hbm,
    sketch_ref, packed_ref,
    send1, recv1, recv1_far, send2, recv2, send3, recv3, gsend, grecv, far_table,
    fields, to_track, wide, pick, far_wide, far_pick, own, incoming, sum_ref,
    send_sems, recv_sems,
    omega_ref, u_ref, w_ref, v_ref, camera_ref, track_ref, mask_ref, load_sems,
):
    track_count, cam_count, params, columns, rows, groups, span = sizes
    devices = track_count * cam_count
    half = devices // 2
    cam_width = omega_ref.shape[1]
    obs_count = camera_ref.shape[1]
    tracks = v_ref.shape[2]
    part_rows = span * rows
    chunk = groups * part_rows
    chunks = half // span
    me = lax.axis_index("track") * cam_count + lax.axis_index("cam")
    side = me // half
    place_at = me - side * half
    home = side * half
    away = half - home

    def where(device):
        return (device // cam_count, lax.rem(device, cam_count))

    def turned_place(turn):
        return lax.rem(place_at + turn, half)

    loads = [
        pltpu.make_async_copy(source, target, load_sems.at[index])
        for index, (source, target) in enumerate(
            [
                (camera_hbm, camera_ref),
                (track_hbm, track_ref),
                (mask_hbm, mask_ref),
                (w_hbm, w_ref),
                (omega_hbm, omega_ref),
                (u_hbm, u_ref),
                (v_hbm, v_ref),
            ]
        )
    ]
    for load in loads:
        load.start()

    barrier = pltpu.get_barrier_semaphore()
    pl.semaphore_signal(
        barrier, inc=1, device_id=where(away + place_at), device_id_type=MESH
    )

    @pl.loop(1, half)
    def _(turn):
        pl.semaphore_signal(
            barrier, inc=1, device_id=where(home + turned_place(turn)), device_id_type=MESH
        )

    def remote(index, src, dst, device):
        return pltpu.make_async_remote_copy(
            src_ref=src,
            dst_ref=dst,
            send_sem=send_sems.at[index],
            recv_sem=recv_sems.at[index],
            device_id=where(device),
            device_id_type=MESH,
        )

    def to_home(index, src, dst):
        @pl.loop(1, half)
        def _(turn):
            other = turned_place(turn)
            remote(index, src.at[other], dst.at[place_at], home + other).start()

        pltpu.make_async_copy(src.at[place_at], dst.at[place_at], recv_sems.at[index]).start()

    def to_away(index, src, dst):
        @pl.loop(0, half)
        def _(turn):
            other = turned_place(turn)
            remote(index, src(other), dst.at[place_at], away + other).start()

    def arrive(index, dst):
        pltpu.make_async_copy(dst, dst, recv_sems.at[index]).wait()

    def sent(index, part):
        pltpu.make_async_copy(part, part, send_sems.at[index]).wait()

    eye = one_hot(rows_iota((LANES, LANES)) == lanes_iota((LANES, LANES)))

    def pack(part, values, dst, at=0):
        for index in range(values.shape[0] // columns):
            block = values[index * columns : (index + 1) * columns]
            pieces = [block[:, g * part_rows : (g + 1) * part_rows] for g in range(groups)]
            if groups * columns < LANES:
                pieces.append(jnp.zeros((LANES - groups * columns, part_rows), F32))
            turned = jnp.concatenate(pieces, axis=0).T.reshape(span, rows, LANES)
            low = at + index * rows
            dst[pl.ds(part * span, span), low : low + rows] = turned.astype(BF16)

    def unpack(part, src, at, count):
        blocks = []
        for index in range(count):
            low = at + index * rows
            block = src[pl.ds(part * span, span), low : low + rows]
            turned = dot_nt(eye, block.reshape(part_rows, LANES))
            blocks.append(
                jnp.concatenate(
                    [turned[g * columns : (g + 1) * columns] for g in range(groups)], axis=1
                )
            )
        return jnp.concatenate(blocks, axis=0)

    with jax.named_scope("place"):
        for load in loads[:4]:
            load.wait()
        camera = camera_ref[...]
        owner = camera // cam_width
        local = camera - owner * cam_width
        owner = owner - home
        owner = jnp.where(owner < 0, owner + devices, owner)
        track_id = lanes_iota((1, obs_count)) // BLK_OBS * TRK_BLK + track_ref[...]
        live = mask_ref[...].astype(F32)
        fields[...] = jnp.zeros_like(fields)
        for row in range(params):
            fields[3 * row : 3 * row + 3, :] = w_ref[row].astype(F32) * live
        high = local // 256
        fields[3 * params : 3 * params + 1, :] = high.astype(F32)
        fields[3 * params + 1 : 3 * params + 2, :] = (local - high * 256).astype(F32)
        owned = one_hot(rows_iota((devices, obs_count)) == owner)
        earlier = one_hot(rows_iota((obs_count, obs_count)) < lanes_iota((obs_count, obs_count)))
        ranks = dot(owned, earlier)
        rank = jnp.sum(ranks * owned.astype(F32), axis=0, keepdims=True).astype(jnp.int32)
        group = jnp.zeros_like(rank)
        for g in range(1, groups):
            group += jnp.where(rank >= g * rows, 1, 0)
        offset = group * part_rows + rank - group * rows
        member = one_hot(rows_iota((tracks, obs_count)) == track_id)
        table = jnp.concatenate([fields[...].astype(BF16), member], axis=0)

        for far in range(2):

            def place(part):
                nearby = owner - far * half - part * span
                inside = jnp.logical_and(nearby >= 0, nearby < span)
                slot = jnp.where(inside, nearby * rows + offset, -1)
                slots = one_hot(rows_iota((chunk, obs_count)) == slot)
                placed = dot_nt(table, slots)
                pack(part, placed[:columns], send1, far * rows)
                to_track[far, part] = placed[columns:].astype(BF16)

            repeat(chunks, place)

    with jax.named_scope("barrier"):
        loads[4].wait()
        pl.semaphore_wait(barrier, half)
    table_copy = remote(TABLE, omega_ref, far_table, away + place_at)
    table_copy.start()
    to_home(ASK, send1, recv1)

    with jax.named_scope("own"):
        for load in loads[5:]:
            load.wait()
        for row in range(params):
            total = jnp.zeros((columns, cam_width), F32)
            for col in range(params):
                total += u_ref[row, col : col + 1, :] * omega_ref[
                    col * columns : (col + 1) * columns, :
                ].astype(F32)
            own[row * columns : (row + 1) * columns, :] = total
        incoming[...] = jnp.zeros_like(incoming)
        sum_ref[...] = jnp.zeros_like(sum_ref)

    def read_request(part, src, at, wide_to, pick_to):
        turned = unpack(part, src, at, 1)
        wide_to[part] = turned
        number = turned[3 * params : 3 * params + 1] * 256.0 + turned[
            3 * params + 1 : 3 * params + 2
        ]
        pick_to[part] = one_hot(rows_iota((cam_width, chunk)) == number.astype(jnp.int32))

    def project(part, cameras, weights, chosen, dst):
        gathered = dot(cameras[...], chosen[part])
        turned = weights[part]
        pieces = []
        for comp in range(3):
            total = jnp.zeros((columns, chunk), F32)
            for row in range(params):
                at = row * 3 + comp
                total += turned[at : at + 1] * gathered[row * columns : (row + 1) * columns]
            pieces.append(total)
        pack(part, jnp.concatenate(pieces, axis=0), dst)

    with jax.named_scope("wait_ask"):
        arrive(ASK, recv1)
    with jax.named_scope("project"):
        repeat(chunks, lambda part: read_request(part, recv1, 0, wide.at[0], pick.at[0]))
        repeat(chunks, lambda part: project(part, omega_ref, wide.at[0], pick.at[0], send2.at[0]))
    to_home(SUM, send2.at[0], recv2.at[0])
    to_away(ASK_FAR, lambda other: send1.at[other, pl.ds(rows, rows)], recv1_far)
    with jax.named_scope("read_far"):
        repeat(chunks, lambda part: read_request(part, recv1, rows, far_wide, far_pick))
    with jax.named_scope("wait_table"):
        arrive(TABLE, far_table)
    with jax.named_scope("project_far"):
        repeat(chunks, lambda part: project(part, far_table, far_wide, far_pick, send2.at[1]))
    to_home(SUM_FAR, send2.at[1], recv2.at[1])

    def collect(far, part):
        values = unpack(part, recv2.at[far], 0, 3).astype(BF16)
        sum_ref[...] += dot_nt(values, to_track[far, part])

    with jax.named_scope("wait_sum"):
        arrive(SUM, recv2.at[0])
    with jax.named_scope("collect"):
        repeat(chunks, lambda part: collect(0, part))
    with jax.named_scope("wait_sum_far"):
        arrive(SUM_FAR, recv2.at[1])
    with jax.named_scope("collect_far"):
        repeat(chunks, lambda part: collect(1, part))
        pieces = []
        for row in range(3):
            total = jnp.zeros((columns, tracks), F32)
            for col in range(3):
                total += v_ref[row, col : col + 1, :] * sum_ref[
                    col * columns : (col + 1) * columns
                ]
            pieces.append(total)
        solved = jnp.concatenate(pieces, axis=0).astype(BF16)
        repeat(
            chunks, lambda part: pack(part, dot(solved, to_track[1, part]), send3.at[1])
        )
    to_away(BACK_FAR, lambda other: send3.at[1, other], recv3.at[1])
    with jax.named_scope("spread"):
        repeat(
            chunks, lambda part: pack(part, dot(solved, to_track[0, part]), send3.at[0])
        )
    to_home(BACK, send3.at[0], recv3.at[0])
    with jax.named_scope("read_ask_far"):
        arrive(ASK_FAR, recv1_far)
        repeat(chunks, lambda part: read_request(part, recv1_far, 0, wide.at[1], pick.at[1]))

    def gather_back(far, part):
        turned = unpack(part, recv3.at[far], 0, 3)
        weights = wide[far, part]
        pieces = []
        for row in range(params):
            total = jnp.zeros((columns, chunk), F32)
            for comp in range(3):
                at = row * 3 + comp
                total += weights[at : at + 1] * turned[comp * columns : (comp + 1) * columns]
            pieces.append(total)
        contribution = jnp.concatenate(pieces, axis=0).astype(BF16)
        incoming[...] += dot_nt(contribution, pick[far, part])

    with jax.named_scope("wait_back"):
        arrive(BACK, recv3.at[0])
    with jax.named_scope("gather"):
        repeat(chunks, lambda part: gather_back(0, part))
    with jax.named_scope("wait_back_far"):
        arrive(BACK_FAR, recv3.at[1])
    with jax.named_scope("gather_far"):
        repeat(chunks, lambda part: gather_back(1, part))

        sketch = own[...] - incoming[...]
        sketch_ref[...] = sketch
        flat = jnp.concatenate(
            [sketch[row * columns : (row + 1) * columns] for row in range(params)], axis=1
        )
        gram = dot_nt(flat, flat, HIGH)
        folds = LANES // columns
        tall = columns // folds
        gsend[...] = jnp.concatenate(
            [gram[part * tall : (part + 1) * tall] for part in range(folds)], axis=1
        )

    @pl.loop(1, devices)
    def _(turn):
        remote(GRAM, gsend, grecv.at[me], lax.rem(me + turn, devices)).start()

    pltpu.make_async_copy(gsend, grecv.at[me], recv_sems.at[GRAM]).start()
    with jax.named_scope("wait_gram"):
        arrive(GRAM, grecv)
    packed_ref[...] = jnp.sum(grecv[...], axis=0)

    most = pl.ds(0, half - 1)
    sent(ASK, recv1.at[most])
    sent(ASK_FAR, recv1_far)
    sent(TABLE, far_table)
    sent(SUM, recv2.at[0, most])
    sent(SUM_FAR, recv2.at[1, most])
    sent(BACK, recv3.at[0, most])
    sent(BACK_FAR, recv3.at[1])
    sent(GRAM, grecv.at[pl.ds(0, devices - 1)])


def finish(
    sizes,
    sketch_ref, packed_ref,
    sketch_hbm, basis_hbm, factor_hbm,
    basis_ref, factor_ref, sems,
):
    params, columns, height = sizes
    cam_width = sketch_ref.shape[1]
    sketch_copy = pltpu.make_async_copy(sketch_ref, sketch_hbm, sems.at[0])
    sketch_copy.start()
    with jax.named_scope("eliminate"):
        folds = LANES // columns
        packed = packed_ref[...]
        gram = jnp.concatenate(
            [packed[:, part * columns : (part + 1) * columns] for part in range(folds)], axis=0
        ) / height
        strips = columns // STRIP
        unit = jnp.where(
            rows_iota((columns, columns)) == lanes_iota((columns, columns)), 1.0, 0.0
        )
        both = jnp.concatenate([unit, gram], axis=1)
        work = [both[s * STRIP : (s + 1) * STRIP] for s in range(strips)]
        row_ids = rows_iota((STRIP, 1))
        roots = [jnp.zeros((STRIP, LANES), F32) for _ in range(strips)]
        for base in range(strips):
            panel = [
                [
                    jnp.broadcast_to(
                        work[s][:, columns + base * STRIP + j : columns + base * STRIP + j + 1],
                        (STRIP, LANES),
                    )
                    for s in range(strips)
                ]
                for j in range(STRIP)
            ]
            for j in range(STRIP):
                pivot = panel[j][base][j : j + 1]
                inverse = 1.0 / pivot
                roots[base] = jnp.where(row_ids == j, lax.rsqrt(pivot), roots[base])
                for s in range(base, strips):
                    scale = jnp.where(row_ids > j, inverse, 0.0) if s == base else inverse
                    work[s] = work[s] - (panel[j][s] * scale)[:, : 2 * columns] * work[base][
                        j : j + 1
                    ]
                    for later in range(j + 1, STRIP):
                        panel[later][s] = panel[later][s] - (
                            panel[j][s] * panel[later][base][j : j + 1]
                        ) * scale
        done = jnp.concatenate(
            [work[s] * roots[s][:, : 2 * columns] for s in range(strips)], axis=0
        )
        inverse = done[:, :columns]
        on_upper = rows_iota((columns, columns)) <= lanes_iota((columns, columns))
        factor_ref[...] = jnp.where(on_upper, done[:, columns:], 0.0)
    factor_copy = pltpu.make_async_copy(factor_ref, factor_hbm, sems.at[1])
    factor_copy.start()
    with jax.named_scope("basis"):
        flat = jnp.concatenate(
            [sketch_ref[row * columns : (row + 1) * columns] for row in range(params)], axis=1
        )
        basis = dot(inverse, flat, HIGH)
        for row in range(params):
            basis_ref[row * columns : (row + 1) * columns, :] = basis[
                :, row * cam_width : (row + 1) * cam_width
            ]
    basis_copy = pltpu.make_async_copy(basis_ref, basis_hbm, sems.at[2])
    basis_copy.start()
    with jax.named_scope("write"):
        sketch_copy.wait()
        factor_copy.wait()
        basis_copy.wait()


def on_device(omega, u_blocks, w_blocks, v_inverse, obs_camera, obs_track, obs_mask):
    track_count = lax.axis_size("track")
    cam_count = lax.axis_size("cam")
    devices = track_count * cam_count
    half = devices // 2
    columns, params, cam_width = omega.shape
    obs_count = obs_camera.shape[0]
    tracks = v_inverse.shape[2]
    capacity = max(2, 2 * obs_count // devices)
    rows = -(-capacity // (LANES // columns) // 8) * 8
    groups = -(-capacity // rows)
    span = half
    while span * rows * groups > CHUNK and span % 2 == 0:
        span //= 2
    chunk = span * rows * groups
    chunks = half // span

    table = omega.transpose(1, 0, 2).reshape(params * columns, cam_width)
    line = (1, obs_count)
    operands = (
        table,
        u_blocks,
        w_blocks,
        v_inverse,
        obs_camera.reshape(line),
        obs_track.reshape(line),
        obs_mask.reshape(line),
    )
    sizes = (track_count, cam_count, params, columns, rows, groups, span)
    message = pltpu.VMEM((2, half, 3 * rows, LANES), BF16)
    tall = columns * columns // LANES
    wide_shape = (chunks, columns, chunk)
    pick_shape = (chunks, cam_width, chunk)
    whole = jax.ShapeDtypeStruct((params * columns, cam_width), F32)
    square = jax.ShapeDtypeStruct((columns, columns), F32)
    in_vmem = pl.BlockSpec(memory_space=pltpu.VMEM)
    anywhere = pl.BlockSpec(memory_space=pl.ANY)
    sketch, packed = pl.pallas_call(
        functools.partial(kernel, sizes),
        out_shape=(
            pltpu.VMEM((params * columns, cam_width), F32),
            pltpu.VMEM((tall, LANES), F32),
        ),
        in_specs=[anywhere] * 7,
        out_specs=(in_vmem,) * 2,
        scratch_shapes=[
            pltpu.VMEM((half, 2 * rows, LANES), BF16),
            pltpu.VMEM((half, 2 * rows, LANES), BF16),
            pltpu.VMEM((half, rows, LANES), BF16),
        ]
        + [message] * 4
        + [
            pltpu.VMEM((tall, LANES), F32),
            pltpu.VMEM((devices, tall, LANES), F32),
            pltpu.VMEM((params * columns, cam_width), BF16),
            pltpu.VMEM((columns, obs_count), F32),
            pltpu.VMEM((2, chunks, tracks, chunk), BF16),
            pltpu.VMEM((2,) + wide_shape, F32),
            pltpu.VMEM((2,) + pick_shape, BF16),
            pltpu.VMEM(wide_shape, F32),
            pltpu.VMEM(pick_shape, BF16),
            pltpu.VMEM((params * columns, cam_width), F32),
            pltpu.VMEM((params * columns, cam_width), F32),
            pltpu.VMEM((3 * columns, tracks), F32),
            pltpu.SemaphoreType.DMA((8,)),
            pltpu.SemaphoreType.DMA((8,)),
        ]
        + [pltpu.VMEM(array.shape, array.dtype) for array in operands]
        + [pltpu.SemaphoreType.DMA((len(operands),))],
        compiler_params=pltpu.CompilerParams(collective_id=0, has_side_effects=True),
    )(*operands)
    sketch, basis, factor = pl.pallas_call(
        functools.partial(finish, (params, columns, params * cam_width * devices)),
        out_shape=(whole, whole, square),
        in_specs=[in_vmem] * 2,
        out_specs=(anywhere,) * 3,
        scratch_shapes=[
            pltpu.VMEM((params * columns, cam_width), F32),
            pltpu.VMEM((columns, columns), F32),
            pltpu.SemaphoreType.DMA((3,)),
        ],
    )(*(pltpu.with_memory_space_constraint(x, pltpu.VMEM) for x in (sketch, packed)))

    def unfold(array):
        return array.reshape(params, columns, cam_width).transpose(1, 0, 2)

    return (unfold(sketch), unfold(basis), factor)


def solution(mesh):
    spread = P(None, None, ("track", "cam"))
    flat = P(("track", "cam"))
    return jax.shard_map(
        on_device,
        mesh=mesh,
        in_specs=(spread,) * 4 + (flat,) * 3,
        out_specs=(spread, spread, P()),
        check_vma=False,
    )
```

time: 37.7 us -> 31.6 us (0.84)
  Pallas kernels: 35 us -> 30.8 us
  local copies, waits for them, and re-layouts: 1.93 us -> 0 us
    pallas_call x1, Pallas kernels: 35 us -> 28.9 us  [on_device(): pl.pallas_call(functools.partial(kernel, sizes), out_shape=(pltpu.VMEM((p...]
    unnamed x3 -> x0, local copies, waits for them, and re-layouts: 1.93 us -> none
    pallas_call x0 -> x1, Pallas kernels: none -> 1.82 us  [on_device(): pl.pallas_call(functools.partial(finish, (params, columns, params * cam_w...]
where the time goes in v1:
time: 31.6 us; the launch traced here: 31.4 us
  Pallas kernels  30.8 us (97%)
  between operations  0.64 us (2%)
    pallas_call x1, Pallas kernels, on_device(): pl.pallas_call(functools.partial(kernel, sizes), out_shape=(pltpu.VMEM((p...  28.9 us
    pallas_call x1, Pallas kernels, on_device(): pl.pallas_call(functools.partial(finish, (params, columns, params * cam_w...  1.82 us

profile of v1, /device:TPU:0, one launch (start us, length us, event | category | flops | bytes accessed | tf_op | source)
XLA Modules:
  0.0 31.4 jit_solution(10699348158633288444)
XLA Ops:
  0.6 28.9 %shard_map.94 = (f32[288,128]{1,0:T(8,128)S(1)}, f32[8,128]{1,0:T(8,128)S(1)}) custom-call(bf16[288,128]{1,0:T(8,128)(2,1)} %bitcast.12, f32[9,9,128]{2,1,0:T(8,128)} %u_hbm.1, bf16[9,3,512]{2,1,0:T(4,128)(2,1)} %w_hbm.1, f32[3,3,128]{2,1,0:T(4,128)} %v_hbm.1, s32[1,512]{1,0:T(1,128)} %bitcast.13, s32[1,512]{1,0:T(1,128)} %bitcast.14, s32[1,512]{1,0:T(1,128)} %bitcast.15), custom_call_target="tpu_custom_call" | custom-call | tf_op jit(solution)/shard_map/pallas_call | solution.py:458
  29.6 1.8 %shard_map.95 = (f32[288,128]{1,0:T(8,128)}, f32[288,128]{1,0:T(8,128)}, f32[32,32]{1,0:T(8,128)}) custom-call(f32[288,128]{1,0:T(8,128)S(1)} %get-tuple-element.8.sketch_ref, f32[8,128]{1,0:T(8,128)S(1)} %get-tuple-element.9.packed_ref), custom_call_target="tpu_custom_call" | custom-call | tf_op jit(solution)/shard_map/pallas_call | solution.py:492

commit v2 on v1

--- a/solution.py
+++ b/solution.py
@@ -12,9 +12,10 @@
 LANES = 128
 STRIP = 8
 CHUNK = 512
+UNROLL = 32
 
 HIGH = lax.Precision.HIGHEST
-MESH = pl.DeviceIdType.MESH
+LOGICAL = pl.DeviceIdType.LOGICAL
 NT = (((1,), (1,)), ((), ()))
 F32 = jnp.float32
 BF16 = jnp.bfloat16
@@ -40,6 +41,14 @@
 
 def lanes_iota(shape):
     return lax.broadcasted_iota(jnp.int32, shape, 1)
+
+
+def turns(first, count, body):
+    if count - first <= UNROLL:
+        for turn in range(first, count):
+            body(turn)
+    else:
+        pl.loop(first, count)(body)
 
 
 def repeat(count, body):
@@ -47,6 +56,59 @@
         body(0)
     else:
         pl.loop(0, count)(body)
+
+
+def fold(gram):
+    columns = gram.shape[0]
+    middle = columns // 2
+    folds = LANES // columns
+    tall = middle // folds
+    top, bottom = gram[:middle], gram[middle:]
+    first, second = [], []
+    for k in range(folds):
+        first.append(top[k * tall : (k + 1) * tall])
+        piece = bottom[k * tall : (k + 1) * tall]
+        second += [piece[:, middle:], piece[:, :middle]]
+    lane = lanes_iota((tall, LANES))
+    row = rows_iota((tall, LANES)) + lane // columns * tall
+    packed = jnp.where(
+        lax.rem(lane, columns) >= row,
+        jnp.concatenate(first, axis=1),
+        jnp.concatenate(second, axis=1),
+    )
+    shape = (middle, columns)
+    on_diagonal = lanes_iota(shape) == rows_iota(shape) + middle
+    diagonal = jnp.sum(jnp.where(on_diagonal, bottom, 0.0), axis=0, keepdims=True)
+    diagonal = jnp.concatenate([diagonal, jnp.zeros((1, LANES - columns), F32)], axis=1)
+    return jnp.concatenate([packed, diagonal], axis=0)
+
+
+def unfold_gram(packed, columns):
+    middle = columns // 2
+    folds = LANES // columns
+    tall = middle // folds
+    both = jnp.concatenate(
+        [packed[:tall, k * columns : (k + 1) * columns] for k in range(folds)], axis=0
+    )
+    gap = jnp.zeros((tall, middle), F32)
+    moved = jnp.concatenate(
+        [
+            jnp.concatenate([gap, packed[:tall, k * columns : k * columns + middle]], axis=1)
+            for k in range(folds)
+        ],
+        axis=0,
+    )
+    shape = (middle, columns)
+    row, lane = rows_iota(shape), lanes_iota(shape)
+    top = jnp.where(lane >= row, both, 0.0)
+    bottom = jnp.where(lane < row + middle, moved, 0.0)
+    bottom += jnp.where(lane == row + middle, packed[tall : tall + 1, :columns], 0.0)
+    half = jnp.concatenate([top, bottom], axis=0)
+    square = (columns, columns)
+    wide = jnp.concatenate([half, jnp.zeros((columns, LANES - columns), F32)], axis=1)
+    turned = jnp.concatenate([wide] + [jnp.zeros((LANES - columns, LANES), F32)], axis=0).T
+    turned = turned[:columns, :columns]
+    return half + jnp.where(lanes_iota(square) == rows_iota(square), 0.0, turned)
 
 
 def kernel(
@@ -73,11 +135,17 @@
     home = side * half
     away = half - home
 
-    def where(device):
-        return (device // cam_count, lax.rem(device, cam_count))
-
-    def turned_place(turn):
-        return lax.rem(place_at + turn, half)
+    def wrapped(start, turn, count):
+        place = start + turn
+        return jnp.where(place >= count, place - count, place)
+
+    barrier = pltpu.get_barrier_semaphore()
+
+    def greet(device):
+        pl.semaphore_signal(barrier, inc=1, device_id=device, device_id_type=LOGICAL)
+
+    turns(1, half, lambda turn: greet(home + wrapped(place_at, turn, half)))
+    greet(away + place_at)
 
     loads = [
         pltpu.make_async_copy(source, target, load_sems.at[index])
@@ -96,48 +164,38 @@
     for load in loads:
         load.start()
 
-    barrier = pltpu.get_barrier_semaphore()
-    pl.semaphore_signal(
-        barrier, inc=1, device_id=where(away + place_at), device_id_type=MESH
-    )
-
-    @pl.loop(1, half)
-    def _(turn):
-        pl.semaphore_signal(
-            barrier, inc=1, device_id=where(home + turned_place(turn)), device_id_type=MESH
-        )
-
     def remote(index, src, dst, device):
         return pltpu.make_async_remote_copy(
             src_ref=src,
             dst_ref=dst,
             send_sem=send_sems.at[index],
             recv_sem=recv_sems.at[index],
-            device_id=where(device),
-            device_id_type=MESH,
+            device_id=device,
+            device_id_type=LOGICAL,
         )
 
     def to_home(index, src, dst):
-        @pl.loop(1, half)
-        def _(turn):
-            other = turned_place(turn)
+        def send(turn):
+            other = wrapped(place_at, turn, half)
             remote(index, src.at[other], dst.at[place_at], home + other).start()
 
+        turns(1, half, send)
         pltpu.make_async_copy(src.at[place_at], dst.at[place_at], recv_sems.at[index]).start()
 
+    far_first = lax.rem(place_at, half // 2) + (1 - side) * (half // 2)
+
     def to_away(index, src, dst):
-        @pl.loop(0, half)
-        def _(turn):
-            other = turned_place(turn)
+        def send(turn):
+            other = wrapped(far_first, turn, half)
             remote(index, src(other), dst.at[place_at], away + other).start()
+
+        turns(0, half, send)
 
     def arrive(index, dst):
         pltpu.make_async_copy(dst, dst, recv_sems.at[index]).wait()
 
     def sent(index, part):
         pltpu.make_async_copy(part, part, send_sems.at[index]).wait()
-
-    eye = one_hot(rows_iota((LANES, LANES)) == lanes_iota((LANES, LANES)))
 
     def pack(part, values, dst, at=0):
         for index in range(values.shape[0] // columns):
@@ -154,7 +212,7 @@
         for index in range(count):
             low = at + index * rows
             block = src[pl.ds(part * span, span), low : low + rows]
-            turned = dot_nt(eye, block.reshape(part_rows, LANES))
+            turned = block.reshape(part_rows, LANES).astype(F32).T
             blocks.append(
                 jnp.concatenate(
                     [turned[g * columns : (g + 1) * columns] for g in range(groups)], axis=1
@@ -206,8 +264,8 @@
         loads[4].wait()
         pl.semaphore_wait(barrier, half)
     table_copy = remote(TABLE, omega_ref, far_table, away + place_at)
+    to_home(ASK, send1, recv1)
     table_copy.start()
-    to_home(ASK, send1, recv1)
 
     with jax.named_scope("own"):
         for load in loads[5:]:
@@ -248,7 +306,6 @@
         repeat(chunks, lambda part: read_request(part, recv1, 0, wide.at[0], pick.at[0]))
         repeat(chunks, lambda part: project(part, omega_ref, wide.at[0], pick.at[0], send2.at[0]))
     to_home(SUM, send2.at[0], recv2.at[0])
-    to_away(ASK_FAR, lambda other: send1.at[other, pl.ds(rows, rows)], recv1_far)
     with jax.named_scope("read_far"):
         repeat(chunks, lambda part: read_request(part, recv1, rows, far_wide, far_pick))
     with jax.named_scope("wait_table"):
@@ -256,6 +313,7 @@
     with jax.named_scope("project_far"):
         repeat(chunks, lambda part: project(part, far_table, far_wide, far_pick, send2.at[1]))
     to_home(SUM_FAR, send2.at[1], recv2.at[1])
+    to_away(ASK_FAR, lambda other: send1.at[other, pl.ds(rows, rows)], recv1_far)
 
     def collect(far, part):
         values = unpack(part, recv2.at[far], 0, 3).astype(BF16)
@@ -318,17 +376,17 @@
         flat = jnp.concatenate(
             [sketch[row * columns : (row + 1) * columns] for row in range(params)], axis=1
         )
-        gram = dot_nt(flat, flat, HIGH)
-        folds = LANES // columns
-        tall = columns // folds
-        gsend[...] = jnp.concatenate(
-            [gram[part * tall : (part + 1) * tall] for part in range(folds)], axis=1
-        )
-
-    @pl.loop(1, devices)
-    def _(turn):
-        remote(GRAM, gsend, grecv.at[me], lax.rem(me + turn, devices)).start()
-
+        head = flat.astype(BF16)
+        rest = (flat - head.astype(F32)).astype(BF16)
+        parts = jnp.concatenate([head, rest], axis=0)
+        products = dot_nt(parts, head) + dot_nt(parts, rest)
+        gram = products[:columns] + products[columns:]
+        gsend[...] = fold(gram)
+
+    def send_gram(turn):
+        remote(GRAM, gsend, grecv.at[me], wrapped(me, turn, devices)).start()
+
+    turns(1, devices, send_gram)
     pltpu.make_async_copy(gsend, grecv.at[me], recv_sems.at[GRAM]).start()
     with jax.named_scope("wait_gram"):
         arrive(GRAM, grecv)
@@ -356,11 +414,7 @@
     sketch_copy = pltpu.make_async_copy(sketch_ref, sketch_hbm, sems.at[0])
     sketch_copy.start()
     with jax.named_scope("eliminate"):
-        folds = LANES // columns
-        packed = packed_ref[...]
-        gram = jnp.concatenate(
-            [packed[:, part * columns : (part + 1) * columns] for part in range(folds)], axis=0
-        ) / height
+        gram = unfold_gram(packed_ref[...], columns) / height
         strips = columns // STRIP
         unit = jnp.where(
             rows_iota((columns, columns)) == lanes_iota((columns, columns)), 1.0, 0.0
@@ -369,30 +423,49 @@
         work = [both[s * STRIP : (s + 1) * STRIP] for s in range(strips)]
         row_ids = rows_iota((STRIP, 1))
         roots = [jnp.zeros((STRIP, LANES), F32) for _ in range(strips)]
-        for base in range(strips):
-            panel = [
-                [
-                    jnp.broadcast_to(
-                        work[s][:, columns + base * STRIP + j : columns + base * STRIP + j + 1],
-                        (STRIP, LANES),
-                    )
-                    for s in range(strips)
-                ]
+        def spread_columns(first, least):
+            low = columns + first * STRIP
+            return [
+                {
+                    s: jnp.broadcast_to(work[s][:, low + j : low + j + 1], (STRIP, LANES))
+                    for s in range(least, strips)
+                }
                 for j in range(STRIP)
             ]
-            for j in range(STRIP):
-                pivot = panel[j][base][j : j + 1]
-                inverse = 1.0 / pivot
-                roots[base] = jnp.where(row_ids == j, lax.rsqrt(pivot), roots[base])
+
+        panel = spread_columns(0, 0)
+        for base in range(strips):
+            later = spread_columns(base + 1, base) if base + 1 < strips else []
+            for j in range(0, STRIP, 2):
+                a = panel[j][base][j : j + 1]
+                b = panel[j + 1][base][j : j + 1]
+                c = panel[j + 1][base][j + 1 : j + 2]
+                det = a * c - b * b
+                over_det, over_a = 1.0 / det, 1.0 / a
+                roots[base] = jnp.where(row_ids == j, lax.rsqrt(a), roots[base])
+                roots[base] = jnp.where(
+                    row_ids == j + 1, lax.rsqrt(det * over_a), roots[base]
+                )
+                first, second, scale = {}, {}, {}
                 for s in range(base, strips):
-                    scale = jnp.where(row_ids > j, inverse, 0.0) if s == base else inverse
-                    work[s] = work[s] - (panel[j][s] * scale)[:, : 2 * columns] * work[base][
-                        j : j + 1
-                    ]
-                    for later in range(j + 1, STRIP):
-                        panel[later][s] = panel[later][s] - (
-                            panel[j][s] * panel[later][base][j : j + 1]
-                        ) * scale
+                    first[s] = panel[j][s] * c - panel[j + 1][s] * b
+                    second[s] = panel[j + 1][s] * a - panel[j][s] * b
+                    scale[s] = (
+                        jnp.where(row_ids > j + 1, over_det, 0.0) if s == base else over_det
+                    )
+                for column in panel[j + 2 :] + later:
+                    upper, lower = column[base][j : j + 1], column[base][j + 1 : j + 2]
+                    for s in range(base, strips):
+                        column[s] = column[s] - (first[s] * upper + second[s] * lower) * scale[s]
+                upper, lower = work[base][j : j + 1], work[base][j + 1 : j + 2]
+                beside = jnp.where(row_ids == j + 1, b * over_a, 0.0)[:, : 2 * columns]
+                for s in range(base, strips):
+                    step = (first[s] * scale[s])[:, : 2 * columns] * upper
+                    step += (second[s] * scale[s])[:, : 2 * columns] * lower
+                    if s == base:
+                        step += beside * upper
+                    work[s] = work[s] - step
+            panel = later
         done = jnp.concatenate(
             [work[s] * roots[s][:, : 2 * columns] for s in range(strips)], axis=0
         )
@@ -448,7 +521,7 @@
     )
     sizes = (track_count, cam_count, params, columns, rows, groups, span)
     message = pltpu.VMEM((2, half, 3 * rows, LANES), BF16)
-    tall = columns * columns // LANES
+    tall = columns * columns // 2 // LANES + 1
     wide_shape = (chunks, columns, chunk)
     pick_shape = (chunks, cam_width, chunk)
     whole = jax.ShapeDtypeStruct((params * columns, cam_width), F32)

time: 31.6 us -> 30.9 us (0.978)
  Pallas kernels: 30.8 us -> 30.1 us
    pallas_call x1, Pallas kernels: 28.9 us -> 28.3 us  [on_device(): pl.pallas_call(functools.partial(kernel, sizes), out_shape=(pltpu.VMEM((p...]
where the time goes in v2:
time: 30.9 us; the launch traced here: 30.7 us
  Pallas kernels  30.1 us (97%)
  between operations  0.64 us (2%)
    pallas_call x1, Pallas kernels, on_device(): pl.pallas_call(functools.partial(kernel, sizes), out_shape=(pltpu.VMEM((p...  28.3 us
    pallas_call x1, Pallas kernels, on_device(): pl.pallas_call(functools.partial(finish, (params, columns, params * cam_w...  1.79 us

profile of v2, /device:TPU:0, one launch (start us, length us, event | category | flops | bytes accessed | tf_op | source)
XLA Modules:
  0.0 30.7 jit_solution(16595065147884916543)
XLA Ops:
  0.6 28.3 %shard_map.94 = (f32[288,128]{1,0:T(8,128)S(1)}, f32[5,128]{1,0:T(8,128)S(1)}) custom-call(bf16[288,128]{1,0:T(8,128)(2,1)} %bitcast.12, f32[9,9,128]{2,1,0:T(8,128)} %u_hbm.1, bf16[9,3,512]{2,1,0:T(4,128)(2,1)} %w_hbm.1, f32[3,3,128]{2,1,0:T(4,128)} %v_hbm.1, s32[1,512]{1,0:T(1,128)} %bitcast.13, s32[1,512]{1,0:T(1,128)} %bitcast.14, s32[1,512]{1,0:T(1,128)} %bitcast.15), custom_call_target="tpu_custom_call" | custom-call | tf_op jit(solution)/shard_map/pallas_call | solution.py:531
  28.9 1.8 %shard_map.95 = (f32[288,128]{1,0:T(8,128)}, f32[288,128]{1,0:T(8,128)}, f32[32,32]{1,0:T(8,128)}) custom-call(f32[288,128]{1,0:T(8,128)S(1)} %get-tuple-element.8.sketch_ref, f32[5,128]{1,0:T(8,128)S(1)} %get-tuple-element.9.packed_ref), custom_call_target="tpu_custom_call" | custom-call | tf_op jit(solution)/shard_map/pallas_call | solution.py:565

commit v3 on v2

--- a/solution.py
+++ b/solution.py
@@ -14,7 +14,6 @@
 CHUNK = 512
 UNROLL = 32
 
-HIGH = lax.Precision.HIGHEST
 LOGICAL = pl.DeviceIdType.LOGICAL
 NT = (((1,), (1,)), ((), ()))
 F32 = jnp.float32
@@ -116,7 +115,7 @@
     omega_hbm, u_hbm, w_hbm, v_hbm, camera_hbm, track_hbm, mask_hbm,
     sketch_ref, packed_ref,
     send1, recv1, recv1_far, send2, recv2, send3, recv3, gsend, grecv, far_table,
-    fields, to_track, wide, pick, far_wide, far_pick, own, incoming, sum_ref,
+    fields, to_track, wide, pick, far_wide, far_pick, own, sum_ref,
     send_sems, recv_sems,
     omega_ref, u_ref, w_ref, v_ref, camera_ref, track_ref, mask_ref, load_sems,
 ):
@@ -182,11 +181,11 @@
         turns(1, half, send)
         pltpu.make_async_copy(src.at[place_at], dst.at[place_at], recv_sems.at[index]).start()
 
-    far_first = lax.rem(place_at, half // 2) + (1 - side) * (half // 2)
+    near_first = lax.rem(place_at, half // 2) + side * (half // 2)
 
     def to_away(index, src, dst):
         def send(turn):
-            other = wrapped(far_first, turn, half)
+            other = wrapped(near_first, turn, half)
             remote(index, src(other), dst.at[place_at], away + other).start()
 
         turns(0, half, send)
@@ -277,7 +276,6 @@
                     col * columns : (col + 1) * columns, :
                 ].astype(F32)
             own[row * columns : (row + 1) * columns, :] = total
-        incoming[...] = jnp.zeros_like(incoming)
         sum_ref[...] = jnp.zeros_like(sum_ref)
 
     def read_request(part, src, at, wide_to, pick_to):
@@ -304,10 +302,9 @@
         arrive(ASK, recv1)
     with jax.named_scope("project"):
         repeat(chunks, lambda part: read_request(part, recv1, 0, wide.at[0], pick.at[0]))
+        repeat(chunks, lambda part: read_request(part, recv1, rows, far_wide, far_pick))
         repeat(chunks, lambda part: project(part, omega_ref, wide.at[0], pick.at[0], send2.at[0]))
     to_home(SUM, send2.at[0], recv2.at[0])
-    with jax.named_scope("read_far"):
-        repeat(chunks, lambda part: read_request(part, recv1, rows, far_wide, far_pick))
     with jax.named_scope("wait_table"):
         arrive(TABLE, far_table)
     with jax.named_scope("project_far"):
@@ -360,7 +357,7 @@
                 total += weights[at : at + 1] * turned[comp * columns : (comp + 1) * columns]
             pieces.append(total)
         contribution = jnp.concatenate(pieces, axis=0).astype(BF16)
-        incoming[...] += dot_nt(contribution, pick[far, part])
+        own[...] -= dot_nt(contribution, pick[far, part])
 
     with jax.named_scope("wait_back"):
         arrive(BACK, recv3.at[0])
@@ -371,7 +368,7 @@
     with jax.named_scope("gather_far"):
         repeat(chunks, lambda part: gather_back(1, part))
 
-        sketch = own[...] - incoming[...]
+        sketch = own[...]
         sketch_ref[...] = sketch
         flat = jnp.concatenate(
             [sketch[row * columns : (row + 1) * columns] for row in range(params)], axis=1
@@ -379,19 +376,15 @@
         head = flat.astype(BF16)
         rest = (flat - head.astype(F32)).astype(BF16)
         parts = jnp.concatenate([head, rest], axis=0)
-        products = dot_nt(parts, head) + dot_nt(parts, rest)
-        gram = products[:columns] + products[columns:]
-        gsend[...] = fold(gram)
+        products = dot_nt(parts, parts)
+        products = products[:columns] + products[columns:]
+        gsend[...] = fold(products[:, :columns]) + fold(products[:, columns:])
 
     def send_gram(turn):
         remote(GRAM, gsend, grecv.at[me], wrapped(me, turn, devices)).start()
 
     turns(1, devices, send_gram)
     pltpu.make_async_copy(gsend, grecv.at[me], recv_sems.at[GRAM]).start()
-    with jax.named_scope("wait_gram"):
-        arrive(GRAM, grecv)
-    packed_ref[...] = jnp.sum(grecv[...], axis=0)
-
     most = pl.ds(0, half - 1)
     sent(ASK, recv1.at[most])
     sent(ASK_FAR, recv1_far)
@@ -400,6 +393,10 @@
     sent(SUM_FAR, recv2.at[1, most])
     sent(BACK, recv3.at[0, most])
     sent(BACK_FAR, recv3.at[1])
+    with jax.named_scope("wait_gram"):
+        arrive(GRAM, grecv)
+    packed_ref[...] = jnp.sum(grecv[...], axis=0)
+
     sent(GRAM, grecv.at[pl.ds(0, devices - 1)])
 
 
@@ -419,7 +416,7 @@
         unit = jnp.where(
             rows_iota((columns, columns)) == lanes_iota((columns, columns)), 1.0, 0.0
         )
-        both = jnp.concatenate([unit, gram], axis=1)
+        both = jnp.concatenate([unit, gram, unit, unit], axis=1)
         work = [both[s * STRIP : (s + 1) * STRIP] for s in range(strips)]
         row_ids = rows_iota((STRIP, 1))
         roots = [jnp.zeros((STRIP, LANES), F32) for _ in range(strips)]
@@ -458,27 +455,32 @@
                     for s in range(base, strips):
                         column[s] = column[s] - (first[s] * upper + second[s] * lower) * scale[s]
                 upper, lower = work[base][j : j + 1], work[base][j + 1 : j + 2]
-                beside = jnp.where(row_ids == j + 1, b * over_a, 0.0)[:, : 2 * columns]
+                beside = jnp.where(row_ids == j + 1, b * over_a, 0.0)
                 for s in range(base, strips):
-                    step = (first[s] * scale[s])[:, : 2 * columns] * upper
-                    step += (second[s] * scale[s])[:, : 2 * columns] * lower
+                    step = (first[s] * scale[s]) * upper
+                    step += (second[s] * scale[s]) * lower
                     if s == base:
                         step += beside * upper
                     work[s] = work[s] - step
             panel = later
         done = jnp.concatenate(
-            [work[s] * roots[s][:, : 2 * columns] for s in range(strips)], axis=0
-        )
-        inverse = done[:, :columns]
+            [work[s] * roots[s] for s in range(strips)], axis=0
+        )
         on_upper = rows_iota((columns, columns)) <= lanes_iota((columns, columns))
-        factor_ref[...] = jnp.where(on_upper, done[:, columns:], 0.0)
+        factor_ref[...] = jnp.where(on_upper, done[:, columns : 2 * columns], 0.0)
     factor_copy = pltpu.make_async_copy(factor_ref, factor_hbm, sems.at[1])
     factor_copy.start()
     with jax.named_scope("basis"):
         flat = jnp.concatenate(
             [sketch_ref[row * columns : (row + 1) * columns] for row in range(params)], axis=1
         )
-        basis = dot(inverse, flat, HIGH)
+        head = flat.astype(BF16)
+        rest = (flat - head.astype(F32)).astype(BF16)
+        upper = done.astype(BF16)
+        lower = (done - upper.astype(F32)).astype(BF16)
+        left = jnp.where(lanes_iota(done.shape) < 3 * columns, upper, lower)
+        right = jnp.concatenate([head, jnp.zeros_like(head), rest, head], axis=0)
+        basis = dot(left, right)
         for row in range(params):
             basis_ref[row * columns : (row + 1) * columns, :] = basis[
                 :, row * cam_width : (row + 1) * cam_width
@@ -553,7 +555,6 @@
             pltpu.VMEM(wide_shape, F32),
             pltpu.VMEM(pick_shape, BF16),
             pltpu.VMEM((params * columns, cam_width), F32),
-            pltpu.VMEM((params * columns, cam_width), F32),
             pltpu.VMEM((3 * columns, tracks), F32),
             pltpu.SemaphoreType.DMA((8,)),
             pltpu.SemaphoreType.DMA((8,)),

time: 30.9 us -> 30.5 us (0.987)
  Pallas kernels: 30.1 us -> 29.7 us
where the time goes in v3:
time: 30.5 us; the launch traced here: 30.3 us
  Pallas kernels  29.7 us (97%)
  between operations  0.64 us (2%)
    pallas_call x1, Pallas kernels, on_device(): pl.pallas_call(functools.partial(kernel, sizes), out_shape=(pltpu.VMEM((p...  28 us
    pallas_call x1, Pallas kernels, on_device(): pl.pallas_call(functools.partial(finish, (params, columns, params * cam_w...  1.68 us

profile of v3, /device:TPU:0, one launch (start us, length us, event | category | flops | bytes accessed | tf_op | source)
XLA Modules:
  0.0 30.3 jit_solution(10050463389607827790)
XLA Ops:
  0.6 28.0 %shard_map.94 = (f32[288,128]{1,0:T(8,128)S(1)}, f32[5,128]{1,0:T(8,128)S(1)}) custom-call(bf16[288,128]{1,0:T(8,128)(2,1)} %bitcast.12, f32[9,9,128]{2,1,0:T(8,128)} %u_hbm.1, bf16[9,3,512]{2,1,0:T(4,128)(2,1)} %w_hbm.1, f32[3,3,128]{2,1,0:T(4,128)} %v_hbm.1, s32[1,512]{1,0:T(1,128)} %bitcast.13, s32[1,512]{1,0:T(1,128)} %bitcast.14, s32[1,512]{1,0:T(1,128)} %bitcast.15), custom_call_target="tpu_custom_call" | custom-call | tf_op jit(solution)/shard_map/pallas_call | solution.py:533
  28.6 1.7 %shard_map.95 = (f32[288,128]{1,0:T(8,128)}, f32[288,128]{1,0:T(8,128)}, f32[32,32]{1,0:T(8,128)}) custom-call(f32[288,128]{1,0:T(8,128)S(1)} %get-tuple-element.8.sketch_ref, f32[5,128]{1,0:T(8,128)S(1)} %get-tuple-element.9.packed_ref), custom_call_target="tpu_custom_call" | custom-call | tf_op jit(solution)/shard_map/pallas_call | solution.py:566

commit v4 on v3

--- a/solution.py
+++ b/solution.py
@@ -181,11 +181,18 @@
         turns(1, half, send)
         pltpu.make_async_copy(src.at[place_at], dst.at[place_at], recv_sems.at[index]).start()
 
-    near_first = lax.rem(place_at, half // 2) + side * (half // 2)
+    quarter = half // 2 if half % 2 == 0 else half
+    in_quarter = lax.rem(place_at, quarter)
+
+    def far_place(turn):
+        other = wrapped(in_quarter, turn % quarter, quarter)
+        if quarter == half:
+            return other
+        return other + quarter * (1 - side + (2 * side - 1) * (turn // quarter))
 
     def to_away(index, src, dst):
         def send(turn):
-            other = wrapped(near_first, turn, half)
+            other = far_place(turn)
             remote(index, src(other), dst.at[place_at], away + other).start()
 
         turns(0, half, send)
@@ -381,7 +388,8 @@
         gsend[...] = fold(products[:, :columns]) + fold(products[:, columns:])
 
     def send_gram(turn):
-        remote(GRAM, gsend, grecv.at[me], wrapped(me, turn, devices)).start()
+        other = jnp.where(turn - 1 >= me, turn, turn - 1)
+        remote(GRAM, gsend, grecv.at[me], other).start()
 
     turns(1, devices, send_gram)
     pltpu.make_async_copy(gsend, grecv.at[me], recv_sems.at[GRAM]).start()
@@ -432,7 +440,7 @@
 
         panel = spread_columns(0, 0)
         for base in range(strips):
-            later = spread_columns(base + 1, base) if base + 1 < strips else []
+            later = spread_columns(base + 1, base + 1) if base + 1 < strips else []
             for j in range(0, STRIP, 2):
                 a = panel[j][base][j : j + 1]
                 b = panel[j + 1][base][j : j + 1]
@@ -443,22 +451,28 @@
                 roots[base] = jnp.where(
                     row_ids == j + 1, lax.rsqrt(det * over_a), roots[base]
                 )
-                first, second, scale = {}, {}, {}
+                first, second, scale, by_first, by_second = {}, {}, {}, {}, {}
                 for s in range(base, strips):
                     first[s] = panel[j][s] * c - panel[j + 1][s] * b
                     second[s] = panel[j + 1][s] * a - panel[j][s] * b
                     scale[s] = (
                         jnp.where(row_ids > j + 1, over_det, 0.0) if s == base else over_det
                     )
-                for column in panel[j + 2 :] + later:
+                    by_first[s] = first[s] * scale[s]
+                    by_second[s] = second[s] * scale[s]
+                for place, column in enumerate(later):
+                    upper = panel[j][base + 1][place : place + 1]
+                    lower = panel[j + 1][base + 1][place : place + 1]
+                    for s in range(base + 1, strips):
+                        column[s] = column[s] - (by_first[s] * upper + by_second[s] * lower)
+                for column in panel[j + 2 :]:
                     upper, lower = column[base][j : j + 1], column[base][j + 1 : j + 2]
                     for s in range(base, strips):
                         column[s] = column[s] - (first[s] * upper + second[s] * lower) * scale[s]
                 upper, lower = work[base][j : j + 1], work[base][j + 1 : j + 2]
                 beside = jnp.where(row_ids == j + 1, b * over_a, 0.0)
                 for s in range(base, strips):
-                    step = (first[s] * scale[s]) * upper
-                    step += (second[s] * scale[s]) * lower
+                    step = by_first[s] * upper + by_second[s] * lower
                     if s == base:
                         step += beside * upper
                     work[s] = work[s] - step

time: 30.5 us -> 30.1 us (0.987)
  Pallas kernels: 29.7 us -> 29.2 us
    pallas_call x1, Pallas kernels: 28 us -> 27.7 us  [on_device(): pl.pallas_call(functools.partial(kernel, sizes), out_shape=(pltpu.VMEM((p...]
where the time goes in v4:
time: 30.1 us; the launch traced here: 29.9 us
  Pallas kernels  29.2 us (97%)
  between operations  0.64 us (2%)
    pallas_call x1, Pallas kernels, on_device(): pl.pallas_call(functools.partial(kernel, sizes), out_shape=(pltpu.VMEM((p...  27.7 us
    pallas_call x1, Pallas kernels, on_device(): pl.pallas_call(functools.partial(finish, (params, columns, params * cam_w...  1.58 us

profile of v4, /device:TPU:0, one launch (start us, length us, event | category | flops | bytes accessed | tf_op | source)
XLA Modules:
  0.0 29.9 jit_solution(10309856781706239230)
XLA Ops:
  0.6 27.7 %shard_map.94 = (f32[288,128]{1,0:T(8,128)S(1)}, f32[5,128]{1,0:T(8,128)S(1)}) custom-call(bf16[288,128]{1,0:T(8,128)(2,1)} %bitcast.12, f32[9,9,128]{2,1,0:T(8,128)} %u_hbm.1, bf16[9,3,512]{2,1,0:T(4,128)(2,1)} %w_hbm.1, f32[3,3,128]{2,1,0:T(4,128)} %v_hbm.1, s32[1,512]{1,0:T(1,128)} %bitcast.13, s32[1,512]{1,0:T(1,128)} %bitcast.14, s32[1,512]{1,0:T(1,128)} %bitcast.15), custom_call_target="tpu_custom_call" | custom-call | tf_op jit(solution)/shard_map/pallas_call | solution.py:547
  28.3 1.6 %shard_map.95 = (f32[288,128]{1,0:T(8,128)}, f32[288,128]{1,0:T(8,128)}, f32[32,32]{1,0:T(8,128)}) custom-call(f32[288,128]{1,0:T(8,128)S(1)} %get-tuple-element.8.sketch_ref, f32[5,128]{1,0:T(8,128)S(1)} %get-tuple-element.9.packed_ref), custom_call_target="tpu_custom_call" | custom-call | tf_op jit(solution)/shard_map/pallas_call | solution.py:580

commit v5 on v4

--- a/solution.py
+++ b/solution.py
@@ -403,7 +403,11 @@
     sent(BACK_FAR, recv3.at[1])
     with jax.named_scope("wait_gram"):
         arrive(GRAM, grecv)
-    packed_ref[...] = jnp.sum(grecv[...], axis=0)
+    total = grecv[...]
+    while total.shape[0] % 2 == 0:
+        middle = total.shape[0] // 2
+        total = total[:middle] + total[middle:]
+    packed_ref[...] = jnp.sum(total, axis=0)
 
     sent(GRAM, grecv.at[pl.ds(0, devices - 1)])
 
@@ -419,7 +423,7 @@
     sketch_copy = pltpu.make_async_copy(sketch_ref, sketch_hbm, sems.at[0])
     sketch_copy.start()
     with jax.named_scope("eliminate"):
-        gram = unfold_gram(packed_ref[...], columns) / height
+        gram = unfold_gram(packed_ref[...] * (1.0 / height), columns)
         strips = columns // STRIP
         unit = jnp.where(
             rows_iota((columns, columns)) == lanes_iota((columns, columns)), 1.0, 0.0

time: 30.1 us -> 30 us (level)
  no operation moved by 1% of the time
where the time goes in v5:
time: 30 us; the launch traced here: 29.9 us
  Pallas kernels  29.2 us (97%)
  between operations  0.64 us (2%)
    pallas_call x1, Pallas kernels, on_device(): pl.pallas_call(functools.partial(kernel, sizes), out_shape=(pltpu.VMEM((p...  27.6 us
    pallas_call x1, Pallas kernels, on_device(): pl.pallas_call(functools.partial(finish, (params, columns, params * cam_w...  1.58 us

profile of v5, /device:TPU:0, one launch (start us, length us, event | category | flops | bytes accessed | tf_op | source)
XLA Modules:
  0.0 29.9 jit_solution(7729861092772882059)
XLA Ops:
  0.6 27.6 %shard_map.94 = (f32[288,128]{1,0:T(8,128)S(1)}, f32[5,128]{1,0:T(8,128)S(1)}) custom-call(bf16[288,128]{1,0:T(8,128)(2,1)} %bitcast.12, f32[9,9,128]{2,1,0:T(8,128)} %u_hbm.1, bf16[9,3,512]{2,1,0:T(4,128)(2,1)} %w_hbm.1, f32[3,3,128]{2,1,0:T(4,128)} %v_hbm.1, s32[1,512]{1,0:T(1,128)} %bitcast.13, s32[1,512]{1,0:T(1,128)} %bitcast.14, s32[1,512]{1,0:T(1,128)} %bitcast.15), custom_call_target="tpu_custom_call" | custom-call | tf_op jit(solution)/shard_map/pallas_call | solution.py:551
  28.3 1.6 %shard_map.95 = (f32[288,128]{1,0:T(8,128)}, f32[288,128]{1,0:T(8,128)}, f32[32,32]{1,0:T(8,128)}) custom-call(f32[288,128]{1,0:T(8,128)S(1)} %get-tuple-element.8.sketch_ref, f32[5,128]{1,0:T(8,128)S(1)} %get-tuple-element.9.packed_ref), custom_call_target="tpu_custom_call" | custom-call | tf_op jit(solution)/shard_map/pallas_call | solution.py:584
